TPU v7x, 32 devices: a whole 2x2x4 slice. The times are simulated.
32 devices in a mesh: rep: 4 (over y, x), fsdp: 8 (over z, core).
Axes of the slice: x: 2, y: 2, z: 4, core: 2. Of those that a mesh axis runs over, the one named last changes fastest.
Arguments:
- latents: bfloat16 [8, 1024, 1152], P('fsdp', 'rep'), may hold values from -6 to 6
- condition: bfloat16 [8, 1152], P('fsdp'), may hold values from -6 to 6
- adapter_index: int32 [8, 5], P('fsdp'), may hold values from 0 to 7
- weight_mod: bfloat16 [1152, 6912], P('fsdp'), may hold values from -0.1875 to 0.1875
- weight_qkv: bfloat16 [1152, 3456], P('fsdp'), may hold values from -0.1875 to 0.1875
- weight_proj: bfloat16 [1152, 1152], P('fsdp'), may hold values from -3 to 3
- weight_fc1: bfloat16 [1152, 4608], P('fsdp'), may hold values from -0.1875 to 0.1875
- weight_fc2: bfloat16 [4608, 1152], P('fsdp'), may hold values from -0.09375 to 0.09375
- master: float32 [3391488], P('fsdp'), may hold values from -0.25 to 0.25
- moment1: float32 [3391488], P('fsdp'), may hold values from -64 to 64
- moment2: float32 [3391488], P('fsdp'), may hold values from 1 to 1000
- cotangent: bfloat16 [8, 1024, 1152], P('fsdp', 'rep'), may hold values from -6 to 6
Outputs:
- output: bfloat16 [8, 1024, 1152], P('fsdp', 'rep')
- latents_grad: float32 [8, 1024, 1152], P('fsdp', 'rep')
- condition_grad: float32 [8, 1152], P('fsdp')
- new_master: float32 [3391488], P('fsdp')
- new_moment1: float32 [3391488], P('fsdp')
- new_moment2: float32 [3391488], P('fsdp')
- rounded_adapters: bfloat16 [3391488], P('fsdp')
All inputs are finite; a program needn't handle non-finite values.
Results may differ from a plain program's by a relative error of at most 0.03.
The roundings to bfloat16 on the way count: a program that leaves them out, or rounds other values in their place, can miss the bound.
Values may be sent and summed in bfloat16 or wider, within the bound.
A program may use at most 256 MiB of HBM per device.

v0:
```python
import jax
import jax.numpy as jnp
from jax import lax
from jax.sharding import PartitionSpec as P

D = 1152
HEAD_DIM = 72
FF = 4608
RANK = 16
ADAPT = 8
STEP = 3
adapter_scale = 2.0
norm_eps = 1e-06


def adapter_shapes():
    pairs = [(D, 6 * D), (D, 3 * D), (D, D), (D, FF), (FF, D)]
    shapes = []
    for fan_in, fan_out in pairs:
        shapes.append((ADAPT, fan_in, RANK))
        shapes.append((ADAPT, RANK, fan_out))
    return shapes


def unpack(flat):
    tables = []
    offset = 0
    for shape in adapter_shapes():
        count = shape[0] * shape[1] * shape[2]
        tables.append(flat[offset : offset + count].reshape(shape))
        offset = offset + count
    return tables


def norm_modulate(values, shift, scale):
    centred = values - jnp.mean(values, axis=-1, keepdims=True)
    spread = jnp.mean(centred * centred, axis=-1, keepdims=True)
    normed = centred * lax.rsqrt(spread + norm_eps)
    return normed * (1.0 + scale[:, None, :]) + shift[:, None, :]


def gelu_tanh(values):
    return jax.nn.gelu(values, approximate=True)


def shards(
    latents,
    condition,
    adapter_index,
    weight_mod,
    weight_qkv,
    weight_proj,
    weight_fc1,
    weight_fc2,
    master,
    moment1,
    moment2,
    cotangent,
):
    maximal_precision = lax.Precision.HIGHEST
    seqs, tokens, width = latents.shape
    heads = width // HEAD_DIM
    scale = HEAD_DIM ** (-0.5)
    adapters = lax.all_gather(master.astype(jnp.bfloat16), "fsdp", axis=0, tiled=True)
    tables = unpack(adapters)
    select = jax.nn.one_hot(adapter_index, ADAPT, dtype=jnp.float32)
    select_low = select.astype(jnp.bfloat16)
    downs = [
        jnp.einsum(
            "sk,kdr->sdr",
            select_low[:, selected_adapter],
            tables[2 * selected_adapter],
            preferred_element_type=jnp.float32,
        ).astype(jnp.bfloat16)
        for selected_adapter in range(5)
    ]
    raise_factors = [
        jnp.einsum(
            "sk,kro->sro",
            select_low[:, selected_adapter],
            tables[2 * selected_adapter + 1],
            preferred_element_type=jnp.float32,
        ).astype(jnp.bfloat16)
        for selected_adapter in range(5)
    ]

    def adapted(rows_low, weight, selected_adapter):
        inner_lowrank = jnp.einsum(
            "std,sdr->str", rows_low, downs[selected_adapter], preferred_element_type=jnp.float32
        ).astype(jnp.bfloat16)
        additional_term = adapter_scale * jnp.einsum(
            "str,sro->sto",
            inner_lowrank,
            raise_factors[selected_adapter],
            preferred_element_type=jnp.float32,
        )
        return (
            jnp.einsum("std,de->ste", rows_low, weight, preferred_element_type=jnp.float32)
            + additional_term,
            inner_lowrank,
        )

    def adapted_back(grad_low, weight, rows_low, inner_lowrank, selected_adapter):
        raise_gradient = adapter_scale * jnp.einsum(
            "str,sto->sro", inner_lowrank, grad_low, preferred_element_type=jnp.float32
        )
        grad_inner = (
            adapter_scale
            * jnp.einsum(
                "sto,sro->str",
                grad_low,
                raise_factors[selected_adapter],
                preferred_element_type=jnp.float32,
            )
        ).astype(jnp.bfloat16)
        grad_down = jnp.einsum(
            "std,str->sdr", rows_low, grad_inner, preferred_element_type=jnp.float32
        )
        grad_rows = jnp.einsum("ste,de->std", grad_low, weight, preferred_element_type=jnp.float32)
        grad_rows = grad_rows + jnp.einsum(
            "str,sdr->std", grad_inner, downs[selected_adapter], preferred_element_type=jnp.float32
        )
        return (grad_rows, grad_down, raise_gradient)

    cond_full = condition.astype(jnp.float32)
    condition_activated, silu_back = jax.vjp(jax.nn.silu, cond_full)
    silu_low = condition_activated.astype(jnp.bfloat16)
    apply_modulation = jnp.dot(
        silu_low,
        lax.all_gather(weight_mod, "fsdp", axis=0, tiled=True),
        preferred_element_type=jnp.float32,
    )
    inner_modulation = jnp.einsum(
        "sd,sdr->sr", silu_low, downs[0], preferred_element_type=jnp.float32
    ).astype(jnp.bfloat16)
    apply_modulation = apply_modulation + adapter_scale * jnp.einsum(
        "sr,sro->so", inner_modulation, raise_factors[0], preferred_element_type=jnp.float32
    )
    shift_a, scale_a, gate_a, shift_m, scale_m, gate_m = jnp.split(apply_modulation, 6, axis=1)
    attn_weight, proj_weight = (
        lax.all_gather(weight_qkv, "fsdp", axis=0, tiled=True),
        lax.all_gather(weight_proj, "fsdp", axis=0, tiled=True),
    )
    residual_in = latents.astype(jnp.float32)
    first, first_back = jax.vjp(norm_modulate, residual_in, shift_a, scale_a)
    first_low = first.astype(jnp.bfloat16)
    qkv, inner_qkv = adapted(first_low, attn_weight, 1)
    qkv_low = qkv.astype(jnp.bfloat16)
    query = qkv_low[..., :width]
    keys = qkv_low[..., width : 2 * width]
    values = qkv_low[..., 2 * width :]
    keys_all, values_all = (
        lax.all_gather(keys, "rep", axis=1, tiled=True),
        lax.all_gather(values, "rep", axis=1, tiled=True),
    )
    length = keys_all.shape[1]
    latent = 0
    query_heads = query[latent].reshape(tokens, heads, HEAD_DIM)
    key_heads = keys_all[latent].reshape(length, heads, HEAD_DIM)
    value_heads = values_all[latent].reshape(length, heads, HEAD_DIM)
    scores = (
        jnp.einsum("qhe,khe->hqk", query_heads, key_heads, preferred_element_type=jnp.float32)
        * scale
    )
    log_total = jax.nn.logsumexp(scores, axis=-1, keepdims=True)
    probs_low = jnp.exp(scores - log_total).astype(jnp.bfloat16)
    mixed_rows = [
        jnp.einsum(
            "hqk,khe->qhe", probs_low, value_heads, preferred_element_type=jnp.float32
        ).reshape(tokens, width)
    ]
    lse_rows = [log_total]
    mixed_low = jnp.stack(mixed_rows).astype(jnp.bfloat16)
    attn_out, inner_proj = adapted(mixed_low, proj_weight, 2)
    after_attn = residual_in + gate_a[:, None] * attn_out
    expand = lax.all_gather(weight_fc1, "fsdp", axis=0, tiled=True)
    second, second_back = jax.vjp(norm_modulate, after_attn, shift_m, scale_m)
    second_low = second.astype(jnp.bfloat16)
    pre, inner_fc1 = adapted(second_low, expand, 3)
    act, gelu_back = jax.vjp(gelu_tanh, pre)
    act_low = act.astype(jnp.bfloat16)
    contract = lax.all_gather(weight_fc2, "fsdp", axis=0, tiled=True)
    mlp_out, inner_fc2 = adapted(act_low, contract, 4)
    result = after_attn + gate_m[:, None] * mlp_out
    grad_out = cotangent.astype(jnp.float32)
    grad_downs = [None] * 5
    raise_gradient_list = [None] * 5
    d_gate_m = jnp.sum(grad_out * mlp_out, axis=1)
    d_mlp = (grad_out * gate_m[:, None]).astype(jnp.bfloat16)
    d_act, grad_downs[4], raise_gradient_list[4] = adapted_back(
        d_mlp, contract, act_low, inner_fc2, 4
    )
    d_pre = gelu_back(d_act)[0].astype(jnp.bfloat16)
    d_second, grad_downs[3], raise_gradient_list[3] = adapted_back(
        d_pre, expand, second_low, inner_fc1, 3
    )
    d_after, d_shift_m, d_scale_m = second_back(d_second)
    d_after = grad_out + d_after
    d_gate_a = jnp.sum(d_after * attn_out, axis=1)
    d_attn = (d_after * gate_a[:, None]).astype(jnp.bfloat16)
    d_mixed, grad_downs[2], raise_gradient_list[2] = adapted_back(
        d_attn, proj_weight, mixed_low, inner_proj, 2
    )
    d_mixed_low = d_mixed.astype(jnp.bfloat16)
    latent = 0
    query_heads = query[latent].reshape(tokens, heads, HEAD_DIM)
    key_heads = keys_all[latent].reshape(length, heads, HEAD_DIM)
    value_heads = values_all[latent].reshape(length, heads, HEAD_DIM)
    grad_heads = d_mixed_low[latent].reshape(tokens, heads, HEAD_DIM)
    scores = (
        jnp.einsum("qhe,khe->hqk", query_heads, key_heads, preferred_element_type=jnp.float32)
        * scale
    )
    probs = jnp.exp(scores - lse_rows[latent])
    probs_low = probs.astype(jnp.bfloat16)
    d_value_rows = [
        jnp.einsum(
            "hqk,qhe->khe", probs_low, grad_heads, preferred_element_type=jnp.float32
        ).reshape(length, width)
    ]
    d_probs = jnp.einsum(
        "qhe,khe->hqk", grad_heads, value_heads, preferred_element_type=jnp.float32
    )
    centre = jnp.sum(probs * d_probs, axis=-1, keepdims=True)
    d_scores = (probs * (d_probs - centre)).astype(jnp.bfloat16)
    d_query_rows = [
        (
            jnp.einsum("hqk,khe->qhe", d_scores, key_heads, preferred_element_type=jnp.float32)
            * scale
        ).reshape(tokens, width)
    ]
    d_key_rows = [
        (
            jnp.einsum("hqk,qhe->khe", d_scores, query_heads, preferred_element_type=jnp.float32)
            * scale
        ).reshape(length, width)
    ]
    d_keys, d_values = (
        lax.psum_scatter(
            jnp.stack(d_key_rows).astype(jnp.bfloat16), "rep", scatter_dimension=1, tiled=True
        ).astype(jnp.float32),
        lax.psum_scatter(
            jnp.stack(d_value_rows).astype(jnp.bfloat16), "rep", scatter_dimension=1, tiled=True
        ).astype(jnp.float32),
    )
    d_qkv = jnp.concatenate([jnp.stack(d_query_rows), d_keys, d_values], axis=-1).astype(
        jnp.bfloat16
    )
    d_first, grad_downs[1], raise_gradient_list[1] = adapted_back(
        d_qkv, attn_weight, first_low, inner_qkv, 1
    )
    d_input, d_shift_a, d_scale_a = first_back(d_first)
    latents_grad = d_after + d_input
    modulation_partial = jnp.concatenate(
        [d_shift_a, d_scale_a, d_gate_a, d_shift_m, d_scale_m, d_gate_m], axis=1
    )
    raise_modulation = raise_factors[0].astype(jnp.float32)
    down_mod = downs[0].astype(jnp.float32)
    raise_gradient_list[0] = adapter_scale * jnp.einsum(
        "sr,so->sro",
        inner_modulation.astype(jnp.float32),
        modulation_partial,
        precision=maximal_precision,
    )
    inner_portion = adapter_scale * jnp.einsum(
        "gi,gwi->gw", modulation_partial, raise_modulation, precision=maximal_precision
    )
    grad_downs[0] = jnp.einsum(
        "sd,sr->sdr", silu_low.astype(jnp.float32), inner_portion, precision=maximal_precision
    )
    modulation_total = lax.psum(modulation_partial, "rep")
    d_silu = jnp.dot(
        modulation_total,
        lax.all_gather(weight_mod, "fsdp", axis=0, tiled=True).astype(jnp.float32).T,
        precision=maximal_precision,
    )
    inner_combined = adapter_scale * jnp.einsum(
        "gi,gwi->gw", modulation_total, raise_modulation, precision=maximal_precision
    )
    d_silu = d_silu + jnp.einsum(
        "sr,sdr->sd", inner_combined, down_mod, precision=maximal_precision
    )
    condition_grad = silu_back(d_silu)[0]
    pieces = []
    for selected_adapter in range(5):
        pieces.append(
            jnp.einsum(
                "sk,sdr->kdr",
                select[:, selected_adapter],
                grad_downs[selected_adapter],
                precision=maximal_precision,
            ).reshape(-1)
        )
        pieces.append(
            jnp.einsum(
                "sk,sro->kro",
                select[:, selected_adapter],
                raise_gradient_list[selected_adapter],
                precision=maximal_precision,
            ).reshape(-1)
        )
    flat_grad = jnp.concatenate(pieces)
    grad = lax.psum_scatter(
        flat_grad.astype(jnp.bfloat16), "fsdp", scatter_dimension=0, tiled=True
    ).astype(jnp.float32)
    grad = lax.psum(grad, "rep")
    new_moment1 = 0.5 * moment1 + 0.5 * grad
    new_moment2 = 0.5 * moment2 + 0.5 * grad * grad
    first_hat = new_moment1 / (1.0 - 0.5**STEP)
    second_hat = new_moment2 / (1.0 - 0.5**STEP)
    new_master = master - 0.01 * (first_hat / (jnp.sqrt(second_hat) + 1e-08) + 0.1 * master)
    return (
        result.astype(jnp.bfloat16),
        latents_grad,
        condition_grad,
        new_master,
        new_moment1,
        new_moment2,
        new_master.astype(jnp.bfloat16),
    )


def solution(mesh):
    return jax.shard_map(
        shards,
        mesh=mesh,
        in_specs=(
            P("fsdp", "rep", None),
            P("fsdp", None),
            P("fsdp", None),
            P("fsdp", None),
            P("fsdp", None),
            P("fsdp", None),
            P("fsdp", None),
            P("fsdp", None),
            P("fsdp"),
            P("fsdp"),
            P("fsdp"),
            P("fsdp", "rep", None),
        ),
        out_specs=(
            P("fsdp", "rep", None),
            P("fsdp", "rep", None),
            P("fsdp", None),
            P("fsdp"),
            P("fsdp"),
            P("fsdp"),
            P("fsdp"),
        ),
        check_vma=False,
    )
```

profile of v0, /device:TPU:0, one launch (start us, length us, event | category | flops | bytes accessed | tf_op | source)
XLA Modules:
  0.0 1016.1 jit_solution(8816787892493126649)
XLA Ops:
  7.2 2.4 convert_element_type.230
  15.3 66.5 %all-gather.11.cloned.1.call-done = bf16[3391488]{0:T(1024)(128)(2,1)} async-done(((bf16[423936]{0:T(1024)(128)(2,1)}), bf16[3391488]{0:T(1024)(128)(2,1)}) %all-gather.11.cloned.1.call-update) | async-done | bytes 6782992 | tf_op jit(solution)/shard_map/all_gather | solution.py:64
  84.7 2.9 slice.191
  87.7 3.7 reshape.802
  91.3 2.5 fusion.107
  93.9 2.5 slice.165
  96.4 2.5 slice.161
  98.9 2.4 multiply_reduce_fusion.6
  104.7 121.4 %all-gather.9.cloned.1.call-done = bf16[1152,6912]{1,0:T(8,128)(2,1)} async-done(((bf16[144,6912]{1,0:T(8,128)(2,1)}), bf16[1152,6912]{1,0:T(8,128)(2,1)}) %all-gather.9.cloned.1.call-update) | async-done | bytes 15925264 | tf_op jit(solution)/shard_map/all_gather | solution.py:130
  226.1 7.7 convolution_reduce_fusion
  235.7 68.8 %all-gather.13.cloned.1.call-done = bf16[1152,3456]{1,0:T(8,128)(2,1)} async-done(((bf16[144,3456]{1,0:T(8,128)(2,1)}), bf16[1152,3456]{1,0:T(8,128)(2,1)}) %all-gather.13.cloned.1.call-update) | async-done | bytes 7962640 | tf_op jit(solution)/shard_map/all_gather | solution.py:141
  304.5 5.8 fusion.111
  317.7 2.8 fusion.108
  322.1 2.6 slice.177
  324.7 2.5 slice.172
  327.2 8.3 slice.182
  335.4 6.3 multiply_reduce_fusion
  343.9 3.2 multiply_reduce_fusion.3
  347.7 2.1 fusion.38
  352.1 52.9 %all-gather.23.cloned.1.call-done = bf16[4608,1152]{1,0:T(8,128)(2,1)} async-done(((bf16[576,1152]{1,0:T(8,128)(2,1)}), bf16[4608,1152]{1,0:T(8,128)(2,1)}) %all-gather.23.cloned.1.call-update) | async-done | bytes 10616848 | tf_op jit(solution)/shard_map/all_gather | solution.py:182
  405.0 12.3 %fusion.56 = f32[256,4608]{1,0:T(8,128)} fusion(bf16[4608,1152]{1,0:T(8,128)(2,1)} %all-gather.23.cloned.1.call-done, bf16[1,256,1152]{2,1,0:T(8,128)(2,1)S(1)} %copy-done.13, f32[1152]{0:T(1024)S(1)} %get-tuple-element.13), kind=kOutput, calls=%fused_computation.129 | convolution fusion | flops 2718793728 | bytes 15929856 | tf_op jit(solution)/shard_map/ste,de->std/dot_general | solution.py:119
  417.3 25.6 %all-gather.17.cloned.1.call-done = bf16[1,1024,1152]{2,1,0:T(8,128)(2,1)} async-done(((bf16[1,256,1152]{2,1,0:T(8,128)(2,1)}), bf16[1,1024,1152]{2,1,0:T(8,128)(2,1)}) %all-gather.17.cloned.1.call-update) | async-done | bytes 2359312 | tf_op jit(solution)/shard_map/all_gather | solution.py:153
  442.9 4.3 copy.49
  447.2 35.3 %all-gather.15.cloned.1.call-done = bf16[1,1024,1152]{2,1,0:T(8,128)(2,1)} async-done(((bf16[1,256,1152]{2,1,0:T(8,128)(2,1)}), bf16[1,1024,1152]{2,1,0:T(8,128)(2,1)}) %all-gather.15.cloned.1.call-update) | async-done | bytes 2359312 | tf_op jit(solution)/shard_map/all_gather | solution.py:154
  482.6 4.7 copy.47
  487.3 4.2 multiply_reduce_fusion.2
  491.5 3.7 exponential_reduce_fusion
  495.2 2.7 copy-done
  497.9 3.9 convolution_convert_fusion.1
  502.7 15.6 %all-gather.19.cloned.1.call-done = bf16[1152,1152]{1,0:T(8,128)(2,1)} async-done(((bf16[144,1152]{1,0:T(8,128)(2,1)}), bf16[1152,1152]{1,0:T(8,128)(2,1)}) %all-gather.19.cloned.1.call-update) | async-done | bytes 2654224 | tf_op jit(solution)/shard_map/all_gather | solution.py:142
  518.3 2.8 fusion.112
  523.8 95.7 %all-gather.21.cloned.1.call-done = bf16[1152,4608]{1,0:T(8,128)(2,1)} async-done(((bf16[144,4608]{1,0:T(8,128)(2,1)}), bf16[1152,4608]{1,0:T(8,128)(2,1)}) %all-gather.21.cloned.1.call-update) | async-done | bytes 10616848 | tf_op jit(solution)/shard_map/all_gather | solution.py:176
  619.5 5.9 fusion.113
  625.5 2.1 multiply_convert_fusion.7
  627.7 6.4 fusion.11
  636.0 3.2 fusion.115
  647.5 2.1 copy.50
  649.6 10.5 %convolution_convert_fusion = bf16[16,72,1024]{2,1,0:T(8,128)(2,1)} fusion(bf16[256,16,72]{0,2,1:T(8,128)(2,1)} %bitcast.241, f32[16,256,1024]{2,1,0:T(8,128)} %copy-done, f32[16,256]{1,0:T(8,128)S(1)} %log_add_fusion), kind=kOutput, calls=%fused_computation.50 | convolution fusion | flops 617742336 | bytes 19742720 | tf_op jit(solution)/shard_map/hqk,qhe->khe/dot_general | solution.py:217
  660.1 12.9 %multiply_reduce_fusion.1 = (f32[16,256]{1,0:T(8,128)S(1)}, f32[16,256,1024]{2,1,0:T(8,128)}) fusion(f32[16,256,1024]{2,1,0:T(8,128)} %copy-done, f32[16,256]{1,0:T(8,128)S(1)} %log_add_fusion, bf16[256,16,72]{0,2,1:T(8,128)(2,1)} %bitcast.242, bf16[1024,16,72]{0,2,1:T(8,128)(2,1)} %bitcast.232), kind=kOutput, calls=%fused_computation.3 | convolution fusion | flops 620752896 | bytes 36536320 | tf_op jit(solution)/shard_map/qhe,khe->hqk/dot_general | solution.py:221
  673.1 12.3 %multiply_convert_fusion.1 = bf16[16,256,1024]{2,1,0:T(8,128)(2,1)S(1)} fusion(f32[16,256,1024]{2,1,0:T(8,128)} %get-tuple-element.61, f32[16,256,1024]{2,1,0:T(8,128)} %copy-done, f32[16,256]{1,0:T(8,128)S(1)} %get-tuple-element.60, f32[16,256]{1,0:T(8,128)S(1)} %log_add_fusion), kind=kLoop, calls=%fused_computation.2 | loop fusion | flops 20971520 | bytes 41975808 | tf_op jit(solution)/shard_map/convert_element_type | solution.py:225
  685.4 3.5 multiply_convert_fusion.6
  692.4 2.1 reshape.828
  696.5 3.7 reshape.825
  700.9 3.2 multiply_convert_fusion.2
  704.1 3.9 reshape.824
  708.0 3.9 reshape.821
  712.0 2.5 fusion.120
  714.5 5.2 multiply_convert_fusion
  719.8 11.3 %reshape.827 = bf16[589824]{0:T(1024)(128)(2,1)} reshape(bf16[8,4608,16]{2,1,0:T(8,128)(2,1)} %multiply_convert_fusion) | data formatting | bytes 2359296 | tf_op jit(solution)/shard_map/reshape | solution.py:292
  731.0 7.0 fusion.24
  738.1 7.2 fusion.114
  749.6 5.9 fusion.101
  759.6 4.0 fusion.33
  768.1 3.6 reshape.816
  771.9 3.5 multiply_convert_fusion.4
  775.4 3.5 reshape.818
  778.9 2.2 reshape.815
  782.8 2.9 constant_dynamic-update-slice_fusion.15
  794.5 142.3 %all-reduce.6.cloned.1.call-done = bf16[3391488]{0:T(1024)(128)(2,1)} async-done(((bf16[3391488]{0:T(1024)(128)(2,1)}), bf16[3391488]{0:T(1024)(128)(2,1)}) %all-reduce.6.cloned.1.call-update) | async-done | bytes 6782992
  936.8 2.4 dynamic-slice_convert_fusion
  939.3 16.9 %psum.14 = f32[6912]{0:T(1024)S(1)} all-reduce(f32[6912]{0:T(1024)S(1)} %copy-done.55), channel_id=1, replica_groups=mesh['rep'=4,'fsdp'=8] {'rep'}, use_global_device_ids=true, to_apply=%region_19.20 | all-reduce | flops 6912 | bytes 55296 | tf_op jit(solution)/shard_map/psum | solution.py:271
  957.0 15.4 %convolution_reduce_fusion.3 = f32[1152]{0:T(1024)S(1)} fusion(f32[6912,1]{0,1:T(1,128)S(1)} %reshape.860, bf16[1152,6912]{1,0:T(8,128)(2,1)} %all-gather.9.cloned.1.call-done), kind=kOutput, calls=%fused_computation.110 | convolution fusion | flops 95551488 | bytes 15957504 | tf_op jit(solution)/shard_map/dot_general | solution.py:272
  973.1 30.4 %all-reduce.4.cloned.1.call-done = f32[423936]{0:T(1024)} async-done(((f32[423936]{0:T(1024)}), f32[423936]{0:T(1024)}) %all-reduce.4.cloned.1.call-update) | async-done | bytes 1695760 | tf_op jit(solution)/shard_map/psum | solution.py:306
  1003.6 5.5 fusion.103
  (365 shorter events, 71.2 us)
Async XLA Ops:
  7.2 74.5 %all-gather.11.cloned.1.call-start = ((), (), s32[]{:S(2)}) async-start(), calls=%async_computation.3 | async-start | bytes 7630848 | tf_op jit(solution)/shard_map/all_gather | solution.py:64
  9.7 4.4 copy-start.73
  9.7 216.4 %all-gather.9.cloned.1.call-start = ((), (), s32[]{:S(2)}) async-start(), calls=%async_computation.2 | async-start | bytes 17915904 | tf_op jit(solution)/shard_map/all_gather | solution.py:130
  10.5 294.0 %all-gather.13.cloned.1.call-start = ((), (), s32[]{:S(2)}) async-start(), calls=%async_computation.4 | async-start | bytes 8957952 | tf_op jit(solution)/shard_map/all_gather | solution.py:141
  11.2 393.8 %all-gather.23.cloned.1.call-start = ((), (), s32[]{:S(2)}) async-start(), calls=%async_computation.9 | async-start | bytes 11943936 | tf_op jit(solution)/shard_map/all_gather | solution.py:182
  11.8 431.2 %all-gather.17.cloned.1.call-start = ((), (), s32[]{:S(2)}) async-start(), calls=%async_computation.6 | async-start | bytes 2949120 | tf_op jit(solution)/shard_map/all_gather | solution.py:153
  12.0 222.5 %copy-start.78 = (f32[256]{0:T(256)}, f32[256]{0:T(256)S(1)}, u32[]{:S(2)}) copy-start(f32[256]{0:T(256)S(1)} %broadcast_multiply_fusion.2) | copy-start | bytes 3076
  12.3 72.4 %copy-start.94 = (f32[256]{0:T(256)}, f32[256]{0:T(256)S(1)}, u32[]{:S(2)}) copy-start(f32[256]{0:T(256)S(1)} %fusion.30) | copy-start | bytes 3076
  93.9 5.0 copy-start.111
  96.4 5.0 copy-start.75
  98.9 4.6 copy-start.23
  104.0 206.2 %copy-start.45 = (bf16[1,16,3456]{2,0,1:T(2,128)(2,1)}, bf16[1,16,3456]{2,0,1:T(2,128)(2,1)S(1)}, u32[]{:S(2)}) copy-start(bf16[1,16,3456]{2,0,1:T(2,128)(2,1)S(1)} %fusion.48) | copy-start | bytes 331780
  104.7 130.7 %copy-start.24 = (bf16[1152,16]{1,0:T(8,128)(2,1)}, bf16[1152,16]{1,0:T(8,128)(2,1)S(1)}, u32[]{:S(2)}) copy-start(bf16[1152,16]{1,0:T(8,128)(2,1)S(1)} %multiply_reduce_fusion.5) | copy-start | bytes 110596
  104.7 130.4 %copy-start.86 = (f32[256]{0:T(256)S(1)}, f32[256]{0:T(256)}, u32[]{:S(2)}) copy-start(f32[256]{0:T(256)} %fusion.81) | copy-start | bytes 3076
  234.5 170.5 %copy-start.69 = (f32[1152]{0:T(1024)}, f32[1152]{0:T(1024)S(1)}, u32[]{:S(2)}) copy-start(f32[1152]{0:T(1024)S(1)} %get-tuple-element.13) | copy-start | bytes 13828
  235.4 74.8 %copy-start.16 = (bf16[256,1152]{1,0:T(8,128)(2,1)}, bf16[256,1152]{1,0:T(8,128)(2,1)S(1)}, u32[]{:S(2)}) copy-start(bf16[256,1152]{1,0:T(8,128)(2,1)S(1)} %fusion.53) | copy-start | bytes 1769476
  235.7 74.6 %copy-start.80 = (bf16[256,16]{0,1:T(8,128)(2,1)}, bf16[256,16]{0,1:T(8,128)(2,1)S(1)}, u32[]{:S(2)}) copy-start(bf16[256,16]{0,1:T(8,128)(2,1)S(1)} %convolution_convert_fusion.4) | copy-start | bytes 24580
  311.0 4.6 copy-start.31
  312.3 170.3 %all-gather.15.cloned.1.call-start = ((), (), s32[]{:S(2)}) async-start(), calls=%async_computation.5 | async-start | bytes 2949120 | tf_op jit(solution)/shard_map/all_gather | solution.py:154
  312.8 205.4 %all-gather.19.cloned.1.call-start = ((), (), s32[]{:S(2)}) async-start(), calls=%async_computation.7 | async-start | bytes 2985984 | tf_op jit(solution)/shard_map/all_gather | solution.py:142
  313.6 305.9 %all-gather.21.cloned.1.call-start = ((), (), s32[]{:S(2)}) async-start(), calls=%async_computation.8 | async-start | bytes 11943936 | tf_op jit(solution)/shard_map/all_gather | solution.py:176
  314.3 431.0 %reduce-scatter.5.cloned.1.call-start = ((), (), s32[]{:S(2)}) async-start(), calls=%async_computation.11 | async-start | bytes 2949120 | tf_op jit(solution)/shard_map/reduce_scatter | solution.py:242
  322.0 5.1 copy-start.22
  327.2 8.3 copy-start.109
  335.4 7.3 copy-start.36
  335.4 7.5 copy-start.37
  341.7 5.3 copy-start.108
  342.8 4.3 copy-start.8
  343.0 8.2 copy-start.58
  347.7 154.1 %copy-start.26 = (bf16[1152,16]{1,0:T(8,128)(2,1)}, bf16[1152,16]{1,0:T(8,128)(2,1)S(1)}, u32[]{:S(2)}) copy-start(bf16[1152,16]{1,0:T(8,128)(2,1)S(1)} %multiply_reduce_fusion.4) | copy-start | bytes 110596
  491.4 6.5 copy-start
  491.5 6.4 copy-start.3
  501.8 19.3 %copy-start.11 = (bf16[16,72,256]{2,1,0:T(8,128)(2,1)}, bf16[16,72,256]{2,1,0:T(8,128)(2,1)S(1)}, u32[]{:S(2)}) copy-start(bf16[16,72,256]{2,1,0:T(8,128)(2,1)S(1)} %convolution_convert_fusion.1) | copy-start | bytes 1769476
  523.5 101.9 %copy-start.18 = (bf16[256,1152]{1,0:T(8,128)(2,1)}, bf16[256,1152]{1,0:T(8,128)(2,1)S(1)}, u32[]{:S(2)}) copy-start(bf16[256,1152]{1,0:T(8,128)(2,1)S(1)} %fusion.50) | copy-start | bytes 1769476
  523.8 101.7 %copy-start.43 = (bf16[1,16,4608]{2,0,1:T(2,128)(2,1)S(1)}, bf16[1,16,4608]{2,0,1:T(2,128)(2,1)}, u32[]{:S(2)}) copy-start(bf16[1,16,4608]{2,0,1:T(2,128)(2,1)} %fusion.38) | copy-start | bytes 442372
  625.5 10.4 %slice-start.1 = ((s8[10616832]{0:T(1024)(128)(4,1)}), s8[4194304]{0:T(1024)(128)(4,1)S(1)}, s32[]{:S(2)}) async-start(s8[10616832]{0:T(1024)(128)(4,1)} %bitcast.247), calls=%async_computation.15 | async-start | bytes 8388608
  627.6 15.4 %copy-start.4 = (bf16[256,4608]{1,0:T(8,128)(2,1)}, bf16[256,4608]{1,0:T(8,128)(2,1)S(1)}, u32[]{:S(2)}) copy-start(bf16[256,4608]{1,0:T(8,128)(2,1)S(1)} %get-tuple-element.57) | copy-start | bytes 7077892
  627.6 8.3 slice-start.2
  627.6 8.3 slice-start.3
  634.8 4.5 copy-start.63
  660.1 85.2 %reduce-scatter.3.cloned.1.call-start = ((), (), s32[]{:S(2)}) async-start(), calls=%async_computation.10 | async-start | bytes 2949120 | tf_op jit(solution)/shard_map/reduce_scatter | solution.py:239
  690.7 246.1 %all-reduce.6.cloned.1.call-start = ((), (), s32[]{:S(2)}) async-start(), calls=%async_computation.13 | async-start | bytes 13565952
  691.7 8.5 copy-start.19
  691.7 8.5 copy-start.64
  692.4 8.2 copy-start.12
  692.4 8.2 copy-start.66
  704.1 7.9 copy-start.99
  731.0 7.0 copy-start.5
  738.1 7.3 copy-start.46
  749.6 5.9 copy-start.25
  749.6 5.9 copy-start.57
  749.6 5.9 copy-start.79
  759.5 4.7 copy-start.48
  763.5 4.2 copy-start.101
  782.8 4.6 copy-start.41
  782.8 5.3 copy-start.35
  792.6 146.7 %copy-start.55 = (f32[6912]{0:T(1024)S(1)}, f32[6912]{0:T(1024)}, u32[]{:S(2)}) copy-start(f32[6912]{0:T(1024)} %copy-done.54) | copy-start | bytes 82948
  792.6 163.6 %copy-start.49 = (bf16[1,16,6912]{2,0,1:T(2,128)(2,1)S(1)}, bf16[1,16,6912]{2,0,1:T(2,128)(2,1)}, u32[]{:S(2)}) copy-start(bf16[1,16,6912]{2,0,1:T(2,128)(2,1)} %copy-done.47) | copy-start | bytes 663556
  792.6 163.9 %copy-start.39 = (bf16[1152,16]{1,0:T(8,128)(2,1)S(1)}, bf16[1152,16]{1,0:T(8,128)(2,1)}, u32[]{:S(2)}) copy-start(bf16[1152,16]{1,0:T(8,128)(2,1)} %copy-done.38) | copy-start | bytes 110596
  792.7 210.9 %all-reduce.4.cloned.1.call-start = ((), (), s32[]{:S(2)}) async-start(), calls=%async_computation.12 | async-start | bytes 3391488 | tf_op jit(solution)/shard_map/psum | solution.py:306
  957.0 15.5 %copy-start.74 = (bf16[1,1152]{1,0:T(2,128)(2,1)S(1)}, bf16[1,1152]{1,0:T(2,128)(2,1)}, u32[]{:S(2)}) copy-start(bf16[1,1152]{1,0:T(2,128)(2,1)} %param.13) | copy-start | bytes 6916
  957.0 15.5 %copy-start.76 = (f32[1,1152]{1,0:T(1,128)S(1)}, f32[1,1152]{1,0:T(1,128)}, u32[]{:S(2)}) copy-start(f32[1,1152]{1,0:T(1,128)} %get-tuple-element.24) | copy-start | bytes 13828
  957.0 46.5 %copy-start.10 = (f32[423936]{0:T(1024)S(1)}, f32[423936]{0:T(1024)}, u32[]{:S(2)}) copy-start(f32[423936]{0:T(1024)} %param.20) | copy-start | bytes 5087236
  957.0 46.5 %copy-start.30 = (f32[423936]{0:T(1024)S(1)}, f32[423936]{0:T(1024)}, u32[]{:S(2)}) copy-start(f32[423936]{0:T(1024)} %param.21) | copy-start | bytes 5087236
  (70 other events, 163.3 us)
Sparse Core Ops, SparseCore 0:
  10.2 71.4 all-gather.10
  83.3 142.6 all-gather.8
  227.7 76.6 all-gather.12
  306.0 98.9 all-gather.22
  407.2 35.6 all-gather.16
  445.2 37.3 all-gather.14
  484.2 33.9 all-gather.18
  519.9 99.5 all-gather.20
  660.2 35.6 reduce-scatter.4
  698.8 37.3 reduce-scatter.2
  792.7 144.0 all-reduce.5
  940.4 63.0 all-reduce.3
where the time goes:
time: 1030 us; the launch traced here: 1020 us
  waiting for transfers between devices  658 us (64%)
  matrix products  148 us (14%)
  local copies, waits for them, and re-layouts  109 us (11%)
  other arithmetic  66.9 us (6%)
  blocking collectives  16.9 us (2%)
  between operations  16.7 us (2%)
    unnamed x13, waiting for transfers between devices  146 us
    all_gather x1, waiting for transfers between devices, shards(): lax.all_gather(weight_mod, 'fsdp', axis=0, tiled=True)  121 us
    all_gather x1, waiting for transfers between devices, shards(): expand = lax.all_gather(weight_fc1, 'fsdp', axis=0, tiled=True)  95.7 us
    all_gather x1, waiting for transfers between devices, shards(): lax.all_gather(weight_qkv, 'fsdp', axis=0, tiled=True)  68.8 us
    all_gather x1, waiting for transfers between devices, shards(): lax.all_gather(master.astype(jnp.bfloat16), 'fsdp', axis=0, tiled=True)  66.5 us
    all_gather x1, waiting for transfers between devices, shards(): contract = lax.all_gather(weight_fc2, 'fsdp', axis=0, tiled=True)  52.9 us
    all_gather x1, waiting for transfers between devices, shards(): lax.all_gather(values, 'rep', axis=1, tiled=True)  35.3 us
    slice x13, local copies, waits for them, and re-layouts, unpack(): tables.append(flat[offset:offset + count].reshape(shape))  31.5 us
  transfers between devices with their start and end apart: 12, of which 10 were waited for; matrix products, arithmetic and copies ran while one was open for 22% of the time, Pallas kernels for 0%

commit v1 on v0

--- a/solution.py
+++ b/solution.py
@@ -11,6 +11,19 @@
 STEP = 3
 adapter_scale = 2.0
 norm_eps = 1e-06
+
+
+def ring_gather(x, axis, dim):
+    ways = lax.axis_size(axis)
+    up = [(d, (d + 1) % ways) for d in range(ways)]
+    down = [(d, (d - 1) % ways) for d in range(ways)]
+    earlier, later = ([x], [x])
+    for _ in range(ways // 2):
+        earlier.append(lax.ppermute(earlier[-1], axis, up))
+    for _ in range((ways - 1) // 2):
+        later.append(lax.ppermute(later[-1], axis, down))
+    line = jnp.concatenate([*earlier[::-1], *later[1:]], axis=dim)
+    return jnp.roll(line, (lax.axis_index(axis) - ways // 2) * x.shape[dim], axis=dim)
 
 
 def adapter_shapes():
@@ -150,7 +163,7 @@
     keys = qkv_low[..., width : 2 * width]
     values = qkv_low[..., 2 * width :]
     keys_all, values_all = (
-        lax.all_gather(keys, "rep", axis=1, tiled=True),
+        ring_gather(keys, "rep", 1),
         lax.all_gather(values, "rep", axis=1, tiled=True),
     )
     length = keys_all.shape[1]

time: 1030 us -> 989 us (0.960)
  waiting for transfers between devices: 658 us -> 600 us
    all_gather x1, waiting for transfers between devices: 52.9 us -> 3.34 us  [shards(): contract = lax.all_gather(weight_fc2, 'fsdp', axis=0, tiled=True)]
    ppermute x0 -> x3, waiting for transfers between devices: none -> 40 us  [the longest x2 29.1 us: ring_gather(): earlier.append(lax.ppermute(earlier[-1], axis, up))]
    all_gather x1, waiting for transfers between devices: 35.3 us -> 6.74 us  [shards(): lax.all_gather(values, 'rep', axis=1, tiled=True)]
    all_gather x1 -> x0, waiting for transfers between devices: 25.6 us -> none  [shards(): lax.all_gather(keys, 'rep', axis=1, tiled=True)]
    unnamed x257 -> x258, local copies, waits for them, and re-layouts: 19.4 us -> 22.4 us
    unnamed x13 -> x12, waiting for transfers between devices: 146 us -> 146 us
  transfers between devices with their start and end apart: 12 -> 14, of which waited for: 10 -> 12; matrix products, arithmetic and copies ran while one was open for 22% -> 24% of each run, Pallas kernels for 0% -> 0%
where the time goes in v1:
time: 989 us; the launch traced here: 977 us
  waiting for transfers between devices  600 us (61%)
  matrix products  155 us (16%)
  local copies, waits for them, and re-layouts  116 us (12%)
  other arithmetic  66.9 us (7%)
  blocking collectives  17 us (2%)
  between operations  16.6 us (2%)
    unnamed x12, waiting for transfers between devices  146 us
    all_gather x1, waiting for transfers between devices, shards(): lax.all_gather(weight_mod, 'fsdp', axis=0, tiled=True)  121 us
    all_gather x1, waiting for transfers between devices, shards(): expand = lax.all_gather(weight_fc1, 'fsdp', axis=0, tiled=True)  95.7 us
    all_gather x1, waiting for transfers between devices, shards(): lax.all_gather(weight_qkv, 'fsdp', axis=0, tiled=True)  68.8 us
    all_gather x1, waiting for transfers between devices, shards(): lax.all_gather(master.astype(jnp.bfloat16), 'fsdp', axis=0, tiled=True)  66.4 us
    slice x13, local copies, waits for them, and re-layouts, unpack(): tables.append(flat[offset:offset + count].reshape(shape))  33.7 us
    psum x1, waiting for transfers between devices, shards(): grad = lax.psum(grad, 'rep')  30.5 us
    ppermute x2, waiting for transfers between devices, ring_gather(): earlier.append(lax.ppermute(earlier[-1], axis, up))  29.1 us
  transfers between devices with their start and end apart: 14, of which 12 were waited for; matrix products, arithmetic and copies ran while one was open for 24% of the time, Pallas kernels for 0%

profile of v1, /device:TPU:0, one launch (start us, length us, event | category | flops | bytes accessed | tf_op | source)
XLA Modules:
  0.0 976.9 jit_solution(16137583799815270778)
XLA Ops:
  7.2 2.4 convert_element_type.230
  15.3 66.4 %all-gather.10.cloned.1.call-done = bf16[3391488]{0:T(1024)(128)(2,1)} async-done(((bf16[423936]{0:T(1024)(128)(2,1)}), bf16[3391488]{0:T(1024)(128)(2,1)}) %all-gather.10.cloned.1.call-update) | async-done | bytes 6782992 | tf_op jit(solution)/shard_map/all_gather | solution.py:77
  84.7 2.9 slice.191
  87.6 3.7 reshape.802
  91.3 2.5 fusion.107
  93.9 2.5 slice.165
  96.4 2.5 slice.161
  98.9 2.4 multiply_reduce_fusion.6
  104.7 121.3 %all-gather.8.cloned.1.call-done = bf16[1152,6912]{1,0:T(8,128)(2,1)} async-done(((bf16[144,6912]{1,0:T(8,128)(2,1)}), bf16[1152,6912]{1,0:T(8,128)(2,1)}) %all-gather.8.cloned.1.call-update) | async-done | bytes 15925264 | tf_op jit(solution)/shard_map/all_gather | solution.py:143
  226.1 7.7 convolution_reduce_fusion
  235.7 68.8 %all-gather.12.cloned.1.call-done = bf16[1152,3456]{1,0:T(8,128)(2,1)} async-done(((bf16[144,3456]{1,0:T(8,128)(2,1)}), bf16[1152,3456]{1,0:T(8,128)(2,1)}) %all-gather.12.cloned.1.call-update) | async-done | bytes 7962640 | tf_op jit(solution)/shard_map/all_gather | solution.py:154
  304.5 5.8 fusion.110
  312.5 14.9 %collective-permute-done = bf16[1,256,1152]{2,1,0:T(8,128)(2,1)S(1)} collective-permute-done((bf16[1,256,1152]{2,1,0:T(8,128)(2,1)S(1)}, bf16[1,256,1152]{2,1,0:T(8,128)(2,1)S(1)}, u32[]{:S(2)}, u32[]{:S(2)}) %collective-permute-start) | collective-permute-done | bytes 589856 | tf_op jit(solution)/shard_map/ppermute | solution.py:22
  328.0 2.4 collective-permute-start.2
  330.4 14.2 %collective-permute-done.1 = bf16[1,256,1152]{2,1,0:T(8,128)(2,1)S(1)} collective-permute-done((bf16[1,256,1152]{2,1,0:T(8,128)(2,1)S(1)}, bf16[1,256,1152]{2,1,0:T(8,128)(2,1)S(1)}, u32[]{:S(2)}, u32[]{:S(2)}) %collective-permute-start.1) | collective-permute-done | bytes 589856 | tf_op jit(solution)/shard_map/ppermute | solution.py:22
  344.7 11.0 %collective-permute-done.2 = bf16[1,256,1152]{2,1,0:T(8,128)(2,1)S(1)} collective-permute-done((bf16[1,256,1152]{2,1,0:T(8,128)(2,1)S(1)}, bf16[1,256,1152]{2,1,0:T(8,128)(2,1)S(1)}, u32[]{:S(2)}, u32[]{:S(2)}) %collective-permute-start.2) | collective-permute-done | bytes 589856 | tf_op jit(solution)/shard_map/ppermute | solution.py:24
  364.4 2.8 fusion.108
  368.5 3.8 slice.177
  372.3 3.7 slice.172
  376.0 8.3 slice.182
  384.3 6.3 multiply_reduce_fusion
  394.8 3.2 multiply_reduce_fusion.3
  398.6 2.1 fusion.38
  401.6 3.3 all-gather.20.cloned.1.call-done
  405.0 12.3 %fusion.56 = f32[256,4608]{1,0:T(8,128)} fusion(bf16[4608,1152]{1,0:T(8,128)(2,1)} %all-gather.20.cloned.1.call-done, bf16[1,256,1152]{2,1,0:T(8,128)(2,1)S(1)} %copy-done.12, f32[1152]{0:T(1024)S(1)} %get-tuple-element.13), kind=kOutput, calls=%fused_computation.129 | convolution fusion | flops 2718793728 | bytes 15929856 | tf_op jit(solution)/shard_map/ste,de->std/dot_general | solution.py:132
  418.2 3.3 constant_dynamic-slice_fusion
  421.5 4.5 copy.47
  426.2 4.2 multiply_reduce_fusion.2
  430.4 3.7 exponential_reduce_fusion
  436.2 6.7 all-gather.14.cloned.1.call-done
  442.9 4.3 copy.45
  447.2 8.7 convolution_convert_fusion.1
  456.8 21.7 %all-gather.16.cloned.1.call-done = bf16[1152,1152]{1,0:T(8,128)(2,1)} async-done(((bf16[144,1152]{1,0:T(8,128)(2,1)}), bf16[1152,1152]{1,0:T(8,128)(2,1)}) %all-gather.16.cloned.1.call-update) | async-done | bytes 2654224 | tf_op jit(solution)/shard_map/all_gather | solution.py:155
  478.5 2.8 fusion.111
  484.0 95.7 %all-gather.18.cloned.1.call-done = bf16[1152,4608]{1,0:T(8,128)(2,1)} async-done(((bf16[144,4608]{1,0:T(8,128)(2,1)}), bf16[1152,4608]{1,0:T(8,128)(2,1)}) %all-gather.18.cloned.1.call-update) | async-done | bytes 10616848 | tf_op jit(solution)/shard_map/all_gather | solution.py:189
  579.7 5.9 fusion.112
  587.9 6.8 fusion.11
  596.6 3.2 fusion.114
  610.2 10.5 %convolution_convert_fusion = bf16[16,72,1024]{2,1,0:T(8,128)(2,1)} fusion(bf16[256,16,72]{0,2,1:T(8,128)(2,1)} %bitcast.241, f32[16,256,1024]{2,1,0:T(8,128)} %copy-done, f32[16,256]{1,0:T(8,128)S(1)} %log_add_fusion), kind=kOutput, calls=%fused_computation.50 | convolution fusion | flops 617742336 | bytes 19742720 | tf_op jit(solution)/shard_map/hqk,qhe->khe/dot_general | solution.py:230
  620.8 12.9 %multiply_reduce_fusion.1 = (f32[16,256]{1,0:T(8,128)S(1)}, f32[16,256,1024]{2,1,0:T(8,128)}) fusion(f32[16,256,1024]{2,1,0:T(8,128)} %copy-done, f32[16,256]{1,0:T(8,128)S(1)} %log_add_fusion, bf16[256,16,72]{0,2,1:T(8,128)(2,1)} %bitcast.242, bf16[1024,16,72]{0,2,1:T(8,128)(2,1)} %bitcast.233), kind=kOutput, calls=%fused_computation.3 | convolution fusion | flops 620752896 | bytes 36536320 | tf_op jit(solution)/shard_map/qhe,khe->hqk/dot_general | solution.py:234
  633.7 12.3 %multiply_convert_fusion.1 = bf16[16,256,1024]{2,1,0:T(8,128)(2,1)S(1)} fusion(f32[16,256,1024]{2,1,0:T(8,128)} %get-tuple-element.61, f32[16,256,1024]{2,1,0:T(8,128)} %copy-done, f32[16,256]{1,0:T(8,128)S(1)} %get-tuple-element.60, f32[16,256]{1,0:T(8,128)S(1)} %log_add_fusion), kind=kLoop, calls=%fused_computation.2 | loop fusion | flops 20971520 | bytes 41975808 | tf_op jit(solution)/shard_map/convert_element_type | solution.py:238
  646.0 3.6 multiply_convert_fusion.6
  657.2 3.5 reshape.825
  661.4 3.2 multiply_convert_fusion.2
  664.6 3.9 reshape.824
  668.5 3.9 reshape.821
  672.5 2.6 fusion.119
  675.1 5.3 multiply_convert_fusion
  680.3 11.3 %reshape.827 = bf16[589824]{0:T(1024)(128)(2,1)} reshape(bf16[8,4608,16]{2,1,0:T(8,128)(2,1)} %multiply_convert_fusion) | data formatting | bytes 2359296 | tf_op jit(solution)/shard_map/reshape | solution.py:305
  691.6 7.0 fusion.24
  698.7 7.2 fusion.113
  710.2 5.9 fusion.101
  720.1 4.0 fusion.33
  728.6 3.6 reshape.816
  732.5 3.5 multiply_convert_fusion.4
  736.0 3.5 reshape.818
  739.5 2.2 reshape.815
  743.4 2.9 constant_dynamic-update-slice_fusion.23
  755.2 142.4 %all-reduce.6.cloned.1.call-done = bf16[3391488]{0:T(1024)(128)(2,1)} async-done(((bf16[3391488]{0:T(1024)(128)(2,1)}), bf16[3391488]{0:T(1024)(128)(2,1)}) %all-reduce.6.cloned.1.call-update) | async-done | bytes 6782992
  897.5 2.4 dynamic-slice_convert_fusion
  900.0 17.0 %psum.14 = f32[6912]{0:T(1024)S(1)} all-reduce(f32[6912]{0:T(1024)S(1)} %copy-done.52), channel_id=1, replica_groups=mesh['rep'=4,'fsdp'=8] {'rep'}, use_global_device_ids=true, to_apply=%region_19.20 | all-reduce | flops 6912 | bytes 55296 | tf_op jit(solution)/shard_map/psum | solution.py:284
  917.9 15.4 %convolution_reduce_fusion.3 = f32[1152]{0:T(1024)S(1)} fusion(f32[6912,1]{0,1:T(1,128)S(1)} %reshape.860, bf16[1152,6912]{1,0:T(8,128)(2,1)} %all-gather.8.cloned.1.call-done), kind=kOutput, calls=%fused_computation.110 | convolution fusion | flops 95551488 | bytes 15957504 | tf_op jit(solution)/shard_map/dot_general | solution.py:285
  934.0 30.5 %all-reduce.4.cloned.1.call-done = f32[423936]{0:T(1024)} async-done(((f32[423936]{0:T(1024)}), f32[423936]{0:T(1024)}) %all-reduce.4.cloned.1.call-update) | async-done | bytes 1695760 | tf_op jit(solution)/shard_map/psum | solution.py:319
  964.4 5.5 fusion.103
  (371 shorter events, 85.5 us)
Async XLA Ops:
  7.2 74.5 %all-gather.10.cloned.1.call-start = ((), (), s32[]{:S(2)}) async-start(), calls=%async_computation.3 | async-start | bytes 7630848 | tf_op jit(solution)/shard_map/all_gather | solution.py:77
  9.7 216.4 %all-gather.8.cloned.1.call-start = ((), (), s32[]{:S(2)}) async-start(), calls=%async_computation.2 | async-start | bytes 17915904 | tf_op jit(solution)/shard_map/all_gather | solution.py:143
  10.5 294.0 %all-gather.12.cloned.1.call-start = ((), (), s32[]{:S(2)}) async-start(), calls=%async_computation.4 | async-start | bytes 8957952 | tf_op jit(solution)/shard_map/all_gather | solution.py:154
  11.2 393.8 %all-gather.20.cloned.1.call-start = ((), (), s32[]{:S(2)}) async-start(), calls=%async_computation.8 | async-start | bytes 11943936 | tf_op jit(solution)/shard_map/all_gather | solution.py:195
  11.8 431.2 %all-gather.14.cloned.1.call-start = ((), (), s32[]{:S(2)}) async-start(), calls=%async_computation.5 | async-start | bytes 2949120 | tf_op jit(solution)/shard_map/all_gather | solution.py:167
  12.0 222.5 %copy-start.75 = (f32[256]{0:T(256)}, f32[256]{0:T(256)S(1)}, u32[]{:S(2)}) copy-start(f32[256]{0:T(256)S(1)} %broadcast_multiply_fusion.2) | copy-start | bytes 3076
  12.3 72.4 %copy-start.91 = (f32[256]{0:T(256)}, f32[256]{0:T(256)S(1)}, u32[]{:S(2)}) copy-start(f32[256]{0:T(256)S(1)} %fusion.30) | copy-start | bytes 3076
  93.9 5.0 copy-start.108
  96.4 5.0 copy-start.72
  98.9 4.5 copy-start.22
  104.0 206.2 %copy-start.42 = (bf16[1,16,3456]{2,0,1:T(2,128)(2,1)}, bf16[1,16,3456]{2,0,1:T(2,128)(2,1)S(1)}, u32[]{:S(2)}) copy-start(bf16[1,16,3456]{2,0,1:T(2,128)(2,1)S(1)} %fusion.48) | copy-start | bytes 331780
  104.7 130.7 %copy-start.23 = (bf16[1152,16]{1,0:T(8,128)(2,1)}, bf16[1152,16]{1,0:T(8,128)(2,1)S(1)}, u32[]{:S(2)}) copy-start(bf16[1152,16]{1,0:T(8,128)(2,1)S(1)} %multiply_reduce_fusion.5) | copy-start | bytes 110596
  104.7 130.4 %copy-start.83 = (f32[256]{0:T(256)S(1)}, f32[256]{0:T(256)}, u32[]{:S(2)}) copy-start(f32[256]{0:T(256)} %fusion.81) | copy-start | bytes 3076
  234.5 170.5 %copy-start.66 = (f32[1152]{0:T(1024)}, f32[1152]{0:T(1024)S(1)}, u32[]{:S(2)}) copy-start(f32[1152]{0:T(1024)S(1)} %get-tuple-element.13) | copy-start | bytes 13828
  235.4 74.8 %copy-start.15 = (bf16[256,1152]{1,0:T(8,128)(2,1)}, bf16[256,1152]{1,0:T(8,128)(2,1)S(1)}, u32[]{:S(2)}) copy-start(bf16[256,1152]{1,0:T(8,128)(2,1)S(1)} %fusion.53) | copy-start | bytes 1769476
  235.7 74.6 %copy-start.77 = (bf16[256,16]{0,1:T(8,128)(2,1)}, bf16[256,16]{0,1:T(8,128)(2,1)S(1)}, u32[]{:S(2)}) copy-start(bf16[256,16]{0,1:T(8,128)(2,1)S(1)} %convolution_convert_fusion.4) | copy-start | bytes 24580
  311.0 16.4 %collective-permute-start = (bf16[1,256,1152]{2,1,0:T(8,128)(2,1)S(1)}, bf16[1,256,1152]{2,1,0:T(8,128)(2,1)S(1)}, u32[]{:S(2)}, u32[]{:S(2)}) collective-permute-start(bf16[1,256,1152]{2,1,0:T(8,128)(2,1)S(1)} %slice.196), channel_id=1, source_target_pairs={{0,8},{8,16},{16,24},{24,0},{1,9},{9,17},{17,25},{25,1},{2,10},{10... | collective-permute-start | bytes 1769480 | tf_op jit(solution)/shard_map/ppermute | solution.py:22
  327.4 17.1 %collective-permute-start.1 = (bf16[1,256,1152]{2,1,0:T(8,128)(2,1)S(1)}, bf16[1,256,1152]{2,1,0:T(8,128)(2,1)S(1)}, u32[]{:S(2)}, u32[]{:S(2)}) collective-permute-start(bf16[1,256,1152]{2,1,0:T(8,128)(2,1)S(1)} %collective-permute-done), channel_id=1, source_target_pairs={{0,8},{8,16},{16,24},{24,0},{1,9},{9,17},{17,25},{25,1},{2,10},{10... | collective-permute-start | bytes 1769480 | tf_op jit(solution)/shard_map/ppermute | solution.py:22
  328.0 27.7 %collective-permute-start.2 = (bf16[1,256,1152]{2,1,0:T(8,128)(2,1)S(1)}, bf16[1,256,1152]{2,1,0:T(8,128)(2,1)S(1)}, u32[]{:S(2)}, u32[]{:S(2)}) collective-permute-start(bf16[1,256,1152]{2,1,0:T(8,128)(2,1)S(1)} %slice.196), channel_id=1, source_target_pairs={{0,24},{8,0},{16,8},{24,16},{1,25},{9,1},{17,9},{25,17},{2,26},{10... | collective-permute-start | bytes 1769480 | tf_op jit(solution)/shard_map/ppermute | solution.py:24
  355.9 5.1 copy-start.89
  355.9 5.7 copy-start.86
  355.9 6.3 copy-start.32
  359.3 119.2 %all-gather.16.cloned.1.call-start = ((), (), s32[]{:S(2)}) async-start(), calls=%async_computation.6 | async-start | bytes 2985984 | tf_op jit(solution)/shard_map/all_gather | solution.py:155
  359.8 219.9 %all-gather.18.cloned.1.call-start = ((), (), s32[]{:S(2)}) async-start(), calls=%async_computation.7 | async-start | bytes 11943936 | tf_op jit(solution)/shard_map/all_gather | solution.py:189
  360.6 345.4 %reduce-scatter.5.cloned.1.call-start = ((), (), s32[]{:S(2)}) async-start(), calls=%async_computation.10 | async-start | bytes 2949120 | tf_op jit(solution)/shard_map/reduce_scatter | solution.py:255
  368.5 7.5 copy-start.21
  376.0 8.3 copy-start.106
  390.6 7.4 copy-start.105
  391.6 6.3 copy-start.7
  392.9 7.9 copy-start.55
  398.6 57.3 %copy-start.25 = (bf16[1152,16]{1,0:T(8,128)(2,1)}, bf16[1152,16]{1,0:T(8,128)(2,1)S(1)}, u32[]{:S(2)}) copy-start(bf16[1152,16]{1,0:T(8,128)(2,1)S(1)} %multiply_reduce_fusion.4) | copy-start | bytes 110596
  421.4 4.5 copy-start.29
  430.4 5.8 copy-start
  455.9 25.4 %copy-start.10 = (bf16[16,72,256]{2,1,0:T(8,128)(2,1)}, bf16[16,72,256]{2,1,0:T(8,128)(2,1)S(1)}, u32[]{:S(2)}) copy-start(bf16[16,72,256]{2,1,0:T(8,128)(2,1)S(1)} %convolution_convert_fusion.1) | copy-start | bytes 1769476
  483.7 101.9 %copy-start.17 = (bf16[256,1152]{1,0:T(8,128)(2,1)}, bf16[256,1152]{1,0:T(8,128)(2,1)S(1)}, u32[]{:S(2)}) copy-start(bf16[256,1152]{1,0:T(8,128)(2,1)S(1)} %fusion.50) | copy-start | bytes 1769476
  484.0 101.6 %copy-start.40 = (bf16[1,16,4608]{2,0,1:T(2,128)(2,1)S(1)}, bf16[1,16,4608]{2,0,1:T(2,128)(2,1)}, u32[]{:S(2)}) copy-start(bf16[1,16,4608]{2,0,1:T(2,128)(2,1)} %fusion.38) | copy-start | bytes 442372
  585.7 10.9 %slice-start.1 = ((s8[10616832]{0:T(1024)(128)(4,1)}), s8[4194304]{0:T(1024)(128)(4,1)S(1)}, s32[]{:S(2)}) async-start(s8[10616832]{0:T(1024)(128)(4,1)} %bitcast.247), calls=%async_computation.14 | async-start | bytes 8388608
  587.8 15.8 %copy-start.3 = (bf16[256,4608]{1,0:T(8,128)(2,1)}, bf16[256,4608]{1,0:T(8,128)(2,1)S(1)}, u32[]{:S(2)}) copy-start(bf16[256,4608]{1,0:T(8,128)(2,1)S(1)} %get-tuple-element.57) | copy-start | bytes 7077892
  587.8 8.7 slice-start.2
  587.9 8.7 slice-start.3
  595.4 4.5 copy-start.60
  620.7 85.3 %reduce-scatter.3.cloned.1.call-start = ((), (), s32[]{:S(2)}) async-start(), calls=%async_computation.9 | async-start | bytes 2949120 | tf_op jit(solution)/shard_map/reduce_scatter | solution.py:252
  651.4 246.2 %all-reduce.6.cloned.1.call-start = ((), (), s32[]{:S(2)}) async-start(), calls=%async_computation.12 | async-start | bytes 13565952
  652.4 8.3 copy-start.18
  652.4 8.3 copy-start.61
  653.1 8.0 copy-start.11
  653.1 8.0 copy-start.63
  664.6 7.9 copy-start.96
  691.6 7.0 copy-start.4
  698.7 7.3 copy-start.43
  710.2 5.9 copy-start.24
  710.2 5.9 copy-start.54
  710.2 5.9 copy-start.76
  720.1 4.7 copy-start.45
  743.4 4.7 copy-start.38
  743.4 5.4 copy-start.34
  753.3 146.7 %copy-start.52 = (f32[6912]{0:T(1024)S(1)}, f32[6912]{0:T(1024)}, u32[]{:S(2)}) copy-start(f32[6912]{0:T(1024)} %copy-done.51) | copy-start | bytes 82948
  753.3 163.8 %copy-start.46 = (bf16[1,16,6912]{2,0,1:T(2,128)(2,1)S(1)}, bf16[1,16,6912]{2,0,1:T(2,128)(2,1)}, u32[]{:S(2)}) copy-start(bf16[1,16,6912]{2,0,1:T(2,128)(2,1)} %copy-done.44) | copy-start | bytes 663556
  753.3 164.1 %copy-start.36 = (bf16[1152,16]{1,0:T(8,128)(2,1)S(1)}, bf16[1152,16]{1,0:T(8,128)(2,1)}, u32[]{:S(2)}) copy-start(bf16[1152,16]{1,0:T(8,128)(2,1)} %copy-done.35) | copy-start | bytes 110596
  753.3 211.1 %all-reduce.4.cloned.1.call-start = ((), (), s32[]{:S(2)}) async-start(), calls=%async_computation.11 | async-start | bytes 3391488 | tf_op jit(solution)/shard_map/psum | solution.py:319
  917.8 15.5 %copy-start.71 = (bf16[1,1152]{1,0:T(2,128)(2,1)S(1)}, bf16[1,1152]{1,0:T(2,128)(2,1)}, u32[]{:S(2)}) copy-start(bf16[1,1152]{1,0:T(2,128)(2,1)} %param.13) | copy-start | bytes 6916
  917.8 15.5 %copy-start.73 = (f32[1,1152]{1,0:T(1,128)S(1)}, f32[1,1152]{1,0:T(1,128)}, u32[]{:S(2)}) copy-start(f32[1,1152]{1,0:T(1,128)} %get-tuple-element.24) | copy-start | bytes 13828
  917.8 46.6 %copy-start.9 = (f32[423936]{0:T(1024)S(1)}, f32[423936]{0:T(1024)}, u32[]{:S(2)}) copy-start(f32[423936]{0:T(1024)} %param.20) | copy-start | bytes 5087236
  917.9 46.6 %copy-start.31 = (f32[423936]{0:T(1024)S(1)}, f32[423936]{0:T(1024)}, u32[]{:S(2)}) copy-start(f32[423936]{0:T(1024)} %param.21) | copy-start | bytes 5087236
  (69 other events, 159.8 us)
Sparse Core Ops, SparseCore 0:
  10.2 71.4 all-gather.9
  83.3 142.6 all-gather.7
  227.7 76.6 all-gather.11
  306.0 98.9 all-gather.19
  407.2 35.6 all-gather.13
  444.4 33.9 all-gather.15
  480.1 99.5 all-gather.17
  620.8 35.6 reduce-scatter.4
  659.6 37.3 reduce-scatter.2
  753.4 144.0 all-reduce.5
  901.3 63.0 all-reduce.3
